TPU v7x, 32 devices: a whole 2x2x4 slice. The times are simulated.
32 devices in a mesh: dp: 2 (over core), seq: 8 (over z, x), mp: 2 (over y).
Axes of the slice: x: 2, y: 2, z: 4, core: 2. Of those that a mesh axis runs over, the one named last changes fastest.
Arguments:
- queries: bfloat16 [4, 1024, 4096], P('dp', 'seq', 'mp'), may hold values from -6 to 6
- vision: bfloat16 [4, 640, 4096], P('dp', 'seq'), may hold values from -6 to 6
- key_weight: bfloat16 [4096, 1024], P(None, 'mp'), may hold values from -0.09375 to 0.09375
- value_weight: bfloat16 [4096, 1024], P(None, 'mp'), may hold values from -0.09375 to 0.09375
- query_gain: float32 [128], replicated, may hold values from 0.6 to 6
- key_gain: float32 [128], replicated, may hold values from 0.6 to 6
- out_grad: bfloat16 [4, 1024, 4096], P('dp', 'seq', 'mp'), may hold values from -6 to 6
- tile_count: int32 [4], P('dp'), may hold values from 1 to 4, as said below
Outputs:
- query_grad: bfloat16 [4, 1024, 4096], P('dp', 'seq', 'mp')
- vision_grad: bfloat16 [4, 640, 4096], P('dp', 'seq', 'mp')
- key_weight_grad: float32 [4096, 1024], P(None, 'mp')
- value_weight_grad: float32 [4096, 1024], P(None, 'mp')
Inputs may be any that keep to these rules, and one draw needn't show every extreme that they name: The live vision tokens of sample s are its first tile_count[s] * 160; some sample has 4 tiles and some other sample has 1.
All inputs are finite; a program needn't handle non-finite values.
Results may differ from a plain program's by a relative error of at most 0.03.
The roundings to bfloat16 on the way count: a program that leaves them out, or rounds other values in their place, can miss the bound.
Values may be sent and summed in bfloat16 or wider, within the bound.
A program may use at most 128 MiB of HBM per device.

v0:
```python
import functools

import jax
import jax.numpy as jnp
from jax import lax
from jax.experimental import pallas as pl
from jax.experimental.pallas import tpu as pltpu
from jax.sharding import PartitionSpec as P

MAX_TILES = 4
EPS = 1e-05
NEG = -1e30
CUTS = 4
MESH = pl.DeviceIdType.MESH
VMEM = pltpu.VMEM
F32 = jnp.float32
BF16 = jnp.bfloat16


def norm_back(raw, inverse, gain, upstream):
    weighted = upstream * gain
    return inverse * weighted - raw * inverse * inverse * inverse * jnp.mean(
        weighted * raw, axis=-1, keepdims=True
    )


def inverse_of(raw):
    return lax.rsqrt(jnp.mean(raw * raw, axis=-1, keepdims=True) + EPS)


def seq_of(place, n):
    half = place // (n // 2)
    along = place + half * (n - 1 - 2 * place)
    return 2 * along + half


def place_of(index, n):
    side = index % 2
    along = index // 2
    return along + side * (n - 1 - 2 * along)


def greet(devices):
    barrier = pltpu.get_barrier_semaphore()
    for device in devices:
        pl.semaphore_signal(barrier, inc=1, device_id=device, device_id_type=MESH)
    pl.semaphore_wait(barrier, len(devices))


def mul(left, right, dims):
    return lax.dot_general(left, right, (dims, ((), ())), preferred_element_type=F32)


def remote(source, target, send_sem, recv_sem, device):
    return pltpu.make_async_remote_copy(
        src_ref=source,
        dst_ref=target,
        send_sem=send_sem,
        recv_sem=recv_sem,
        device_id=device,
        device_id_type=MESH,
    )


class Ring:
    def __init__(self, n):
        self.n = n
        self.here = lax.axis_index("seq")
        self.place = place_of(self.here, n)
        self.nexts = (seq_of((self.place + 1) % n, n), seq_of((self.place + n - 1) % n, n))

    def origin(self, way, step):
        n, place = self.n, self.place
        return seq_of((place + n - step) % n if way == 0 else (place + step) % n, n)

    def dest(self, way, step):
        n, place = self.n, self.place
        return seq_of((place + 2 * n - 1 - step) % n if way == 0 else (place + 1 + step) % n, n)


def is_first(step):
    return isinstance(step, int) and step == 0


class Gather:
    def __init__(self, ring, pairs, chunks, source, target, sems, landed=None):
        self.ring, self.pairs, self.chunks = ring, pairs, chunks
        self.source, self.target, self.sems, self.landed = source, target, sems, landed
        self.lane = lax.axis_index("dp")

    def ring_copy(self, way, chunk, step):
        target = self.target(way, chunk, self.lane, self.ring.origin(way, step))
        block = self.source(way, chunk) if is_first(step) else target
        send, recv = self.sems[0].at[way, step, chunk], self.sems[1].at[way, step, chunk]
        return remote(block, target, send, recv, {"seq": self.ring.nexts[way]})

    def pair_copy(self, way, chunk, step, at):
        target = self.target(way, chunk, self.lane, self.ring.origin(way, step))
        block = self.source(way, chunk) if is_first(step) else target
        send, recv = self.sems[2].at[way, step, chunk, at], self.sems[3].at[way, step, chunk, at]
        return remote(block, target, send, recv, {"dp": (self.lane + 1 + at) % self.pairs})

    def start(self, way, chunk, step, last=False):
        if not last:
            self.ring_copy(way, chunk, step).start()
        for at in range(self.pairs - 1):
            self.pair_copy(way, chunk, step, at).start()

    def step(self, chunk, step):
        last = isinstance(step, int) and step == self.ring.n - 1
        for way in range(2):
            self.ring_copy(way, chunk, step - 1).wait_recv()
            self.start(way, chunk, step, last)
        if self.landed is not None:
            for way in range(2):
                self.landed(way, chunk, self.lane, self.ring.origin(way, step))
        self.settle(chunk, step - 1)

    def settle(self, chunk, step):
        for way in range(2):
            for at in range(self.pairs - 1):
                self.pair_copy(way, chunk, step, at).wait_recv()
                if self.landed is not None:
                    whose = (self.lane + self.pairs - 1 - at) % self.pairs
                    self.landed(way, chunk, whose, self.ring.origin(way, step))

    def drain(self):
        n = self.ring.n
        for chunk in range(self.chunks):
            for way in range(2):
                for step in range(n):
                    if step < n - 1:
                        self.ring_copy(way, chunk, step).wait_send()
                    for at in range(self.pairs - 1):
                        self.pair_copy(way, chunk, step, at).wait_send()


def whole_kernel(sizes, group, tile_tokens, tile, tiles_hbm, query_hbm, vision_hbm, key_hbm, value_hbm, query_gain_hbm,
                 key_gain_hbm, grad_hbm, query_out, vision_out, key_weight, value_weight, tiles_ref, query_gain, key_gain, queries,
                 out_grad, vision, own, raw_keys,
                 gathered, parts, held, columns, grads, leaving, arrived, total, every, mine, load_sem, own_sem,
                 push_send, push_recv, mate_send, mate_recv, scatter_send, scatter_recv, leave_sem, arrive_sem, *sems):
    pairs, n, heads_cut = sizes
    ring = Ring(n)
    weights = (key_weight, value_weight)
    here, lane, me = ring.here, lax.axis_index("dp"), lax.axis_index("mp")
    samples, rows, width = vision.shape
    heads, _, text_rows, wide = queries.shape
    head_dim = key_gain.shape[1]
    model_columns = heads * head_dim
    tokens = n * rows
    scale = head_dim ** (-0.5)
    depth = width // CUTS
    shard = columns.shape[-1]
    groups = samples if heads_cut % samples == 0 else 1

    loads = [pltpu.make_async_copy(vision_hbm, vision, load_sem.at[0])]
    for at, source in enumerate((key_hbm, value_hbm)):
        for cut in range(CUTS):
            span = pl.ds(cut * depth, depth)
            loads.append(
                pltpu.make_async_copy(source.at[span], weights[at].at[span], load_sem.at[1 + at * CUTS + cut])
            )
    later = [(key_gain_hbm, key_gain), (query_gain_hbm, query_gain), (tiles_hbm, tiles_ref)]
    for head in range(heads):
        for source, target in ((query_hbm, queries), (grad_hbm, out_grad)):
            later.append((source.at[:, :, head * wide : (head + 1) * wide], target.at[head]))
    for at, (source, target) in enumerate(later):
        loads.append(pltpu.make_async_copy(source, target, load_sem.at[1 + 2 * CUTS + at]))
    for load in loads:
        load.start()

    peers = [((lane + shift // n) % pairs, (here + shift % n) % n) for shift in range(1, pairs * n)]
    mates = [(me + shift) % heads_cut for shift in range(1, heads_cut)]
    greet([{"dp": peer[0], "seq": peer[1]} for peer in peers] + [{"mp": mate} for mate in mates])
    loads[0].wait()

    seat = me % groups
    kept = [seat] if groups > 1 else list(range(samples))

    def columns_of(sample, pair, index, held_in=None):
        held_in = vision if held_in is None else held_in
        return held_in.at[sample, :, pl.ds(pl.multiple_of((pair * n + index) * shard, shard), shard)]

    pushes = [
        remote(
            columns_of(sample, *peer),
            columns.at[lane, sample, here],
            push_send.at[at, shift],
            push_recv.at[at, shift],
            {"dp": peer[0], "seq": peer[1]},
        )
        for at, sample in enumerate(kept)
        for shift, peer in enumerate(peers)
    ]
    for copy in pushes:
        copy.start()
    mine_here = [
        pltpu.make_async_copy(
            columns_of(sample, lane, here, vision_hbm), columns.at[lane, sample, here], own_sem.at[at]
        )
        for at, sample in enumerate(kept)
    ]
    for copy in mine_here:
        copy.start()
    swaps = [
        remote(
            columns.at[pair, seat],
            columns.at[pair, seat],
            mate_send.at[pair, at],
            mate_recv.at[pair, at],
            {"mp": me - seat + (seat + 1 + at) % groups},
        )
        for pair in range(pairs)
        for at in range(groups - 1)
    ]

    gather = Gather(
        ring,
        1,
        samples,
        lambda way, chunk: own.at[way, chunk],
        lambda way, chunk, whose, origin: gathered.at[way, chunk, origin],
        sems[:4],
    )

    def project(at):
        product = None
        for cut in range(CUTS):
            loads[1 + at * CUTS + cut].wait()
            left = vision[:, :, cut * depth : (cut + 1) * depth].reshape(samples * rows, depth)
            part = jnp.dot(left, weights[at][cut * depth : (cut + 1) * depth], preferred_element_type=F32)
            product = part if product is None else product + part
        return product

    product = project(0)
    loads[1 + 2 * CUTS].wait()
    for at in range(heads):
        span = slice(at * head_dim, (at + 1) * head_dim)
        head = product[:, span]
        normed = (head * inverse_of(head) * key_gain[...]).astype(BF16)
        raw_keys[:, at] = head.reshape(samples, rows, head_dim)
        own[0, :, at] = normed.reshape(samples, rows, head_dim)
    gather.start(0, 0, 0)
    product = project(1).astype(BF16)
    for at in range(heads):
        own[1, :, at] = product[:, at * head_dim : (at + 1) * head_dim].reshape(samples, rows, head_dim)
    gather.start(1, 0, 0)
    for at in range(2):
        gathered[at, :, here] = own[at]

    lag = heads
    for step in range(1, n):
        gather.step(0, step)
        if step == lag:
            for way in range(2):
                gather.start(way, 1, 0)
        if lag < step < n - 1:
            gather.step(1, step - lag)

    def attend(sample, head):
        live = tiles_ref[:, sample : sample + 1] * tile_tokens

        def stacked(ref):
            cuts = [ref[head, sample, :, at * head_dim : (at + 1) * head_dim] for at in range(group)]
            return jnp.concatenate(cuts, axis=0)

        raw = stacked(queries).astype(F32)
        outs = stacked(out_grad)
        gain = query_gain[...]
        inverse = inverse_of(raw)
        normed = (raw * inverse * gain).astype(BF16)
        keys = gathered[0, sample, :, head].reshape(tokens, head_dim)
        values = gathered[1, sample, :, head].reshape(tokens, head_dim)
        scores = mul(normed, keys, ((1,), (1,))) * scale
        token = lax.broadcasted_iota(jnp.int32, scores.shape, 1)
        scores = jnp.where(token < live, scores, NEG)
        expo = jnp.exp(scores - jnp.max(scores, axis=-1, keepdims=True))
        probs = expo * (1.0 / jnp.sum(expo, axis=-1, keepdims=True))
        probs_b = probs.astype(BF16)
        attn = mul(probs_b, values, ((1,), (0,))).astype(BF16)
        delta = jnp.sum(outs.astype(F32) * attn.astype(F32), axis=-1, keepdims=True)
        dprobs = mul(outs, values, ((1,), (1,)))
        dscores = (probs * (dprobs - delta)).astype(BF16)
        value_part = mul(probs_b, outs, ((0,), (0,))).astype(BF16)
        key_part = (mul(dscores, normed, ((0,), (0,))) * scale).astype(BF16)
        parts[0, sample, :, head] = key_part.reshape(n, rows, head_dim)
        parts[1, sample, :, head] = value_part.reshape(n, rows, head_dim)
        dnormed = mul(dscores, keys, ((1,), (0,))) * scale
        back = norm_back(raw, inverse, gain, dnormed).astype(BF16)
        for at in range(group):
            cut = slice(at * head_dim, (at + 1) * head_dim)
            query_out[head, sample, :, cut] = back[at * text_rows : (at + 1) * text_rows]

    def scatter_copy(way, chunk, step, block=None):
        block = held.at[way, chunk, step] if block is None else block
        send, recv = scatter_send.at[way, step, chunk], scatter_recv.at[way, step, chunk]
        return remote(block, held.at[way, chunk, step], send, recv, {"seq": ring.nexts[way]})

    def scatter_start(chunk):
        for way in range(2):
            scatter_copy(way, chunk, 0, parts.at[way, chunk, ring.dest(way, 0)]).start()

    def scatter_sum(way, chunk, step):
        scatter_copy(way, chunk, step - 1).wait_recv()
        return held[way, chunk, step - 1].astype(F32) + parts[way, chunk, ring.dest(way, step)].astype(F32)

    def scatter_step(chunk, step):
        for way in range(2):
            held[way, chunk, step - 1] = scatter_sum(way, chunk, step).astype(BF16)
            scatter_copy(way, chunk, step, held.at[way, chunk, step - 1]).start()

    def scatter_last(chunk):
        summed = scatter_sum(0, chunk, n - 1)
        values = scatter_sum(1, chunk, n - 1)
        gain = key_gain[...]
        for at in range(heads):
            cut = slice(at * head_dim, (at + 1) * head_dim)
            raw = raw_keys[chunk, at]
            grads[0, chunk, :, cut] = norm_back(raw, inverse_of(raw), gain, summed[at]).astype(BF16)
            grads[1, chunk, :, cut] = values[at].astype(BF16)

    for load in loads[2 + 2 * CUTS :]:
        load.wait()

    def first_sample(head, carry):
        gather.step(1, n - 1 - lag + head)
        attend(0, head)
        return carry

    lax.fori_loop(0, heads, first_sample, 0)
    scatter_start(0)
    gather.step(1, n - 1)
    for copy in pushes:
        copy.wait_recv()
    for copy in mine_here:
        copy.wait()
    for copy in swaps:
        copy.start()

    def second_sample(head, carry):
        scatter_step(0, head + 1)
        attend(1, head)
        return carry

    lax.fori_loop(0, heads, second_sample, 0)
    scatter_start(1)

    spread = Gather(
        ring,
        pairs,
        samples,
        lambda way, chunk: grads.at[way, chunk],
        lambda way, chunk, whose, origin: every.at[way, whose, chunk, origin],
        sems[4:8],
    )
    for step in range(heads + 1, n):
        if step < n - 1:
            scatter_step(0, step)
        else:
            scatter_last(0)
            for way in range(2):
                spread.start(way, 0, 0)
        scatter_step(1, step - heads)
    for step in range(1, heads):
        spread.step(0, step)
        scatter_step(1, n - 1 - heads + step)
    spread.step(0, heads)
    scatter_last(1)
    for way in range(2):
        spread.start(way, 1, 0)
        every[way, lane, :, here] = grads[way]

    share = total.shape[1]
    tiles = share // tile
    copies = []

    def vision_part(owner, at):
        span = pl.ds(pl.multiple_of(owner * share + at * tile, tile), tile)
        part = None
        for kind in range(2):
            left = grads[kind].reshape(samples * rows, model_columns)
            term = mul(left, weights[kind][span, :], ((1,), (1,)))
            part = term if part is None else part + term
        return part

    def leave(at):
        copy = remote(leaving.at[at], arrived.at[at], leave_sem.at[at], arrive_sem.at[at], {"mp": mates[at]})
        copy.start()
        copies.append(copy)

    jobs = []
    for turn, owner in enumerate(mates + [me]):
        for at in range(tiles):

            def job(turn=turn, owner=owner, at=at):
                span = slice(at * tile, (at + 1) * tile)
                part = vision_part(owner, at)
                if turn == len(mates):
                    total[:, span] = part
                    return
                leaving[turn, :, span] = part.astype(BF16)
                if at == tiles - 1:
                    leave(turn)

            jobs.append(job)

    plan = []
    for step in range(heads + 1, n):
        plan.append((0, step))
        plan.append((1, step - heads))
    for step in range(n - heads, n - 1):
        plan.append((1, step))
    per_step = -(-len(jobs) // (len(plan) - 1))
    for chunk, step in plan:
        for _ in range(min(per_step, len(jobs))):
            jobs.pop(0)()
        spread.step(chunk, step)
    for job in jobs:
        job()
    spread.step(1, n - 1)
    for chunk in range(samples):
        spread.settle(chunk, n - 1)

    half = shard // 2

    def rows_of(whose, origin, way):
        return pl.ds(pl.multiple_of(((whose * n + origin) * 2 + way) * half, half), half)

    share_out = Gather(
        ring,
        pairs,
        2,
        lambda way, chunk: mine.at[chunk, way],
        lambda way, chunk, whose, origin: weights[chunk].at[rows_of(whose, origin, way)],
        sems[8:],
    )
    for copy in swaps:
        copy.wait()
    for chunk in range(2):
        grad = mul(
            columns[...].reshape(pairs * samples * tokens, shard),
            every[chunk].reshape(pairs * samples * tokens, model_columns),
            ((0,), (0,)),
        ).astype(BF16)
        mine[chunk] = grad.reshape(mine.shape[1:])
        for way in range(2):
            share_out.start(way, chunk, 0)
    result = total[...]
    for at, copy in enumerate(copies):
        copy.wait()
        result = result + arrived[at].astype(F32)
    vision_out[...] = result.astype(BF16)
    for chunk in range(2):
        for way in range(2):
            weights[chunk][rows_of(lane, here, way), :] = mine[chunk, way]
    for step in range(1, n):
        for chunk in range(2):
            share_out.step(chunk, step)
    for chunk in range(2):
        share_out.settle(chunk, n - 1)

    for copy in pushes:
        copy.wait_send()
    for chunk in range(samples):
        for way in range(2):
            for step in range(n - 1):
                scatter_copy(way, chunk, step).wait_send()
    for each in (gather, spread, share_out):
        each.drain()


def emit_kernel(query_ref, vision_ref, key_ref, value_ref, query_out, vision_out, key_out, value_out, staged, sem, own_sem):
    heads, _, _, wide = query_ref.shape
    passed = [pltpu.make_async_copy(vision_ref, vision_out, own_sem.at[heads])]
    for at in range(heads):
        passed.append(
            pltpu.make_async_copy(
                query_ref.at[at], query_out.at[:, :, at * wide : (at + 1) * wide], own_sem.at[at]
            )
        )
    slots, block = staged.shape[:2]
    blocks = key_out.shape[0] // block
    copies = []
    for at in range(2 * blocks):
        kind, span = at // blocks, pl.ds(at % blocks * block, block)
        slot = at % slots
        if at >= slots:
            copies[at - slots].wait()
        staged[slot] = (key_ref, value_ref)[kind][span, :].astype(F32)
        copy = pltpu.make_async_copy(staged.at[slot], (key_out, value_out)[kind].at[span], sem.at[slot])
        copy.start()
        copies.append(copy)
        if at < len(passed):
            passed[at].start()
    for copy in copies[-slots:] + passed:
        copy.wait()


def emit(query_grad, vision_grad, key_grad, value_grad):
    rows, columns = key_grad.shape
    heads, samples, text_rows, wide = query_grad.shape
    grad = jax.ShapeDtypeStruct((rows, columns), F32)
    block = rows // 16
    dma = pltpu.SemaphoreType.DMA
    return pl.pallas_call(
        emit_kernel,
        out_shape=(
            jax.ShapeDtypeStruct((samples, text_rows, heads * wide), BF16),
            jax.ShapeDtypeStruct(vision_grad.shape, BF16),
            grad,
            grad,
        ),
        in_specs=[pl.BlockSpec(memory_space=VMEM)] * 4,
        out_specs=(pl.BlockSpec(memory_space=pltpu.HBM),) * 4,
        scratch_shapes=[VMEM((4, block, columns), F32), dma((4,)), dma((heads + 1,))],
        compiler_params=pltpu.CompilerParams(vmem_limit_bytes=16 * 1024 * 1024),
        cost_estimate=pl.CostEstimate(flops=2 * rows * columns, bytes_accessed=8 * rows * columns, transcendentals=0),
        name="emit",
    )(query_grad, vision_grad, key_grad, value_grad)


def ring_sems(n, pairs, chunks):
    dma = pltpu.SemaphoreType.DMA
    pair = dma((2, n, chunks, max(pairs - 1, 1)))
    return [dma((2, n, chunks)), dma((2, n, chunks)), pair, pair]


def in_hbm(array):
    return pltpu.with_memory_space_constraint(array, pltpu.HBM)


def local(sizes, queries, vision, key_weight, value_weight, query_gain, key_gain, out_grad, tile_count):
    pairs, n, heads_cut = sizes
    samples, rows, width = vision.shape
    columns = key_weight.shape[1]
    head_dim = key_gain.shape[0]
    heads = columns // head_dim
    group = queries.shape[2] // columns
    block = (heads, rows, head_dim)
    by_head = (heads, samples, queries.shape[1], group * head_dim)
    share = width // heads_cut
    shard = width // (pairs * n)
    groups = samples if heads_cut % samples == 0 else 1
    kept = 1 if groups > 1 else samples
    tile = 512 if share % 512 == 0 else share
    moved = VMEM((max(heads_cut - 1, 1), samples * rows, share), BF16)
    dma = pltpu.SemaphoreType.DMA
    hbm = pl.BlockSpec(memory_space=pltpu.HBM)
    vmem = pl.BlockSpec(memory_space=VMEM)
    sent = 6 * samples * (n - 1) * rows * columns * 2 + 2 * (n - 1) * shard * columns * 2
    whole = pl.pallas_call(
        functools.partial(whole_kernel, sizes, group, n * rows // MAX_TILES, tile),
        out_shape=(
            jax.ShapeDtypeStruct(by_head, BF16),
            jax.ShapeDtypeStruct((samples * rows, share), BF16),
            jax.ShapeDtypeStruct((width, columns), BF16),
            jax.ShapeDtypeStruct((width, columns), BF16),
        ),
        in_specs=[hbm] * 8,
        out_specs=(vmem,) * 4,
        scratch_shapes=[
            VMEM((1, samples), jnp.int32),
            VMEM((1, head_dim), F32),
            VMEM((1, head_dim), F32),
            VMEM(by_head, BF16),
            VMEM(by_head, BF16),
            VMEM(vision.shape, BF16),
            VMEM((2, samples, *block), BF16),
            VMEM((samples, *block), F32),
            VMEM((2, samples, n, *block), BF16),
            VMEM((2, samples, n, *block), BF16),
            VMEM((2, samples, n - 1, *block), BF16),
            VMEM((pairs, samples, n, rows, shard), BF16),
            VMEM((2, samples, rows, columns), BF16),
            moved,
            moved,
            VMEM((samples * rows, share), F32),
            VMEM((2, pairs, samples, n, rows, columns), BF16),
            VMEM((2, 2, shard // 2, columns), BF16),
            dma((4 + 2 * CUTS + 2 * heads,)),
            dma((kept,)),
            dma((kept, pairs * n)),
            dma((kept, pairs * n)),
            dma((pairs, max(groups - 1, 1))),
            dma((pairs, max(groups - 1, 1))),
            dma((2, n, samples)),
            dma((2, n, samples)),
            dma((max(heads_cut - 1, 1),)),
            dma((max(heads_cut - 1, 1),)),
        ]
        + ring_sems(n, 1, samples)
        + ring_sems(n, pairs, samples)
        + ring_sems(n, pairs, 2),
        compiler_params=pltpu.CompilerParams(
            collective_id=1, has_side_effects=True, vmem_limit_bytes=LIMIT
        ),
        cost_estimate=pl.CostEstimate(flops=25_000_000_000, bytes_accessed=sent, transcendentals=0),
        name="whole",
    )(
        *map(
            in_hbm,
            (
                tile_count[None],
                queries,
                vision,
                key_weight,
                value_weight,
                query_gain[None],
                key_gain[None],
                out_grad,
            ),
        )
    )
    query_grad, vision_grad, key_grad, value_grad = emit(*whole)
    return query_grad, vision_grad.reshape(samples, rows, share), key_grad, value_grad


LIMIT = 38 * 1024 * 1024


def solution(mesh):
    sizes = (mesh.shape["dp"], mesh.shape["seq"], mesh.shape["mp"])
    in_specs = (
        P("dp", "seq", "mp"),
        P("dp", "seq", None),
        P(None, "mp"),
        P(None, "mp"),
        P(),
        P(),
        P("dp", "seq", "mp"),
        P("dp"),
    )
    out_specs = (P("dp", "seq", "mp"), P("dp", "seq", "mp"), P(None, "mp"), P(None, "mp"))
    return jax.shard_map(
        functools.partial(local, sizes), mesh=mesh, in_specs=in_specs, out_specs=out_specs, check_vma=False
    )
```

profile of v0, /device:TPU:0, one launch (start us, length us, event | category | flops | bytes accessed | tf_op | source)
XLA Modules:
  0.0 188.6 jit_solution(7925626120593945244)
XLA Ops:
  0.6 180.4 %whole.1 = (bf16[4,2,128,512]{3,2,1,0:T(8,128)(2,1)S(1)}, bf16[160,2048]{1,0:T(8,128)(2,1)S(1)}, bf16[4096,512]{1,0:T(8,128)(2,1)S(1)}, bf16[4096,512]{1,0:T(8,128)(2,1)S(1)}) custom-call(s32[1,2]{1,0:T(1,128)} %bitcast.5, bf16[2,128,2048]{2,1,0:T(8,128)(2,1)} %query_hbm.1, bf16[2,80,4096]{2,1,0:T(8,128)(2,1)} %vision_hbm.1, bf16[4096,512]{1,0:T(8,128)(2,1)} %key_hbm.1, ...), custom_call_target="tpu_custom_call" | custom-call | flops 24999999488 | bytes 10551296 | tf_op jit(solution)/shard_map/whole/pallas_call | solution.py:552
  181.0 7.7 %emit.1 = (bf16[2,128,2048]{2,1,0:T(8,128)(2,1)}, bf16[160,2048]{1,0:T(8,128)(2,1)}, f32[4096,512]{1,0:T(8,128)}, f32[4096,512]{1,0:T(8,128)}) custom-call(bf16[4,2,128,512]{3,2,1,0:T(8,128)(2,1)S(1)} %get-tuple-element.12.query_ref, bf16[160,2048]{1,0:T(8,128)(2,1)S(1)} %get-tuple-element.13.vision_ref, bf16[4096,512]{1,0:T(8,128)(2,1)S(1)} %get-tuple-element.14.key_ref, ...), custom_call_target="tpu_custom_call" | custom-call | flops 4194304 | bytes 16777216 | tf_op jit(solution)/shard_map/emit/pallas_call | solution.py:506
where the time goes:
time: 189 us
  Pallas kernels  188 us (99%)
    pallas_call x1, Pallas kernels, local(): pl.pallas_call(functools.partial(whole_kernel, sizes, group, n * rows //...  180 us
    pallas_call x1, Pallas kernels, emit(): pl.pallas_call(emit_kernel, out_shape=(jax.ShapeDtypeStruct((samples, tex...  7.65 us

commit v1 on v0

--- a/solution.py
+++ b/solution.py
@@ -11,6 +11,7 @@
 EPS = 1e-05
 NEG = -1e30
 CUTS = 4
+EARLY_PUSHES = 7
 MESH = pl.DeviceIdType.MESH
 VMEM = pltpu.VMEM
 F32 = jnp.float32
@@ -44,7 +45,7 @@
     barrier = pltpu.get_barrier_semaphore()
     for device in devices:
         pl.semaphore_signal(barrier, inc=1, device_id=device, device_id_type=MESH)
-    pl.semaphore_wait(barrier, len(devices))
+    return lambda: pl.semaphore_wait(barrier, len(devices))
 
 
 def mul(left, right, dims):
@@ -73,9 +74,23 @@
         n, place = self.n, self.place
         return seq_of((place + n - step) % n if way == 0 else (place + step) % n, n)
 
-    def dest(self, way, step):
+    def dest(self, way, away):
         n, place = self.n, self.place
-        return seq_of((place + 2 * n - 1 - step) % n if way == 0 else (place + 1 + step) % n, n)
+        return seq_of((place + away) % n if way == 0 else (place + n - away) % n, n)
+
+    def reach(self, way, kind):
+        return self.n // 2 if way == kind else self.n - 1 - self.n // 2
+
+
+def when(step, below, most=None):
+    def run(body):
+        known = step if isinstance(step, int) else most
+        if known is not None and known < below:
+            body()
+        elif not isinstance(step, int):
+            pl.when(step < below)(body)
+
+    return run
 
 
 def is_first(step):
@@ -83,62 +98,82 @@
 
 
 class Gather:
-    def __init__(self, ring, pairs, chunks, source, target, sems, landed=None):
-        self.ring, self.pairs, self.chunks = ring, pairs, chunks
-        self.source, self.target, self.sems, self.landed = source, target, sems, landed
+    def __init__(self, ring, pairs, chunks, cuts, source, target, sems):
+        self.ring, self.pairs, self.chunks, self.cuts = ring, pairs, chunks, cuts
+        self.source, self.target, self.sems = source, target, sems
         self.lane = lax.axis_index("dp")
 
-    def ring_copy(self, way, chunk, step):
-        target = self.target(way, chunk, self.lane, self.ring.origin(way, step))
-        block = self.source(way, chunk) if is_first(step) else target
-        send, recv = self.sems[0].at[way, step, chunk], self.sems[1].at[way, step, chunk]
-        return remote(block, target, send, recv, {"seq": self.ring.nexts[way]})
-
-    def pair_copy(self, way, chunk, step, at):
-        target = self.target(way, chunk, self.lane, self.ring.origin(way, step))
-        block = self.source(way, chunk) if is_first(step) else target
-        send, recv = self.sems[2].at[way, step, chunk, at], self.sems[3].at[way, step, chunk, at]
-        return remote(block, target, send, recv, {"dp": (self.lane + 1 + at) % self.pairs})
-
-    def start(self, way, chunk, step, last=False):
-        if not last:
-            self.ring_copy(way, chunk, step).start()
-        for at in range(self.pairs - 1):
-            self.pair_copy(way, chunk, step, at).start()
-
-    def step(self, chunk, step):
-        last = isinstance(step, int) and step == self.ring.n - 1
-        for way in range(2):
-            self.ring_copy(way, chunk, step - 1).wait_recv()
-            self.start(way, chunk, step, last)
-        if self.landed is not None:
-            for way in range(2):
-                self.landed(way, chunk, self.lane, self.ring.origin(way, step))
-        self.settle(chunk, step - 1)
-
-    def settle(self, chunk, step):
-        for way in range(2):
-            for at in range(self.pairs - 1):
-                self.pair_copy(way, chunk, step, at).wait_recv()
-                if self.landed is not None:
-                    whose = (self.lane + self.pairs - 1 - at) % self.pairs
-                    self.landed(way, chunk, whose, self.ring.origin(way, step))
+    def block(self, way, kind, chunk, step, cut):
+        target = self.target(kind, chunk, self.lane, self.ring.origin(way, step), cut)
+        return self.source(kind, chunk, cut) if is_first(step) else target, target
+
+    def ring_copy(self, way, kind, chunk, step, cut):
+        at = (way, step, kind * self.chunks + chunk, cut)
+        block = self.block(way, kind, chunk, step, cut)
+        return remote(*block, self.sems[0].at[at], self.sems[1].at[at], {"seq": self.ring.nexts[way]})
+
+    def pair_copy(self, way, kind, chunk, step, cut, turn):
+        at = (way, step, kind * self.chunks + chunk, cut, turn)
+        block = self.block(way, kind, chunk, step, cut)
+        other = {"dp": (self.lane + 1 + turn) % self.pairs}
+        return remote(*block, self.sems[2].at[at], self.sems[3].at[at], other)
+
+    def send(self, way, kind, chunk, step, cut, most=None):
+        @when(step, self.ring.reach(way, kind), most)
+        def _():
+            self.ring_copy(way, kind, chunk, step, cut).start()
+
+        if not is_first(step) or way == kind:
+            for turn in range(self.pairs - 1):
+                self.pair_copy(way, kind, chunk, step, cut, turn).start()
+
+    def start(self, chunk, kinds=(0, 1)):
+        for cut in range(self.cuts):
+            for kind in kinds:
+                for way in range(2):
+                    self.send(way, kind, chunk, 0, cut)
+
+    def step(self, chunk, step, cuts=None, most=None):
+        for cut in range(self.cuts) if cuts is None else cuts:
+            for kind in range(2):
+                for way in range(2):
+
+                    @when(step, self.ring.reach(way, kind) + 1, most)
+                    def _():
+                        self.ring_copy(way, kind, chunk, step - 1, cut).wait_recv()
+                        self.send(way, kind, chunk, step, cut, most)
+
+    def parcels(self):
+        for chunk in range(self.chunks):
+            for kind in range(2):
+                for way in range(2):
+                    for cut in range(self.cuts):
+                        yield way, kind, chunk, cut
+
+    def pair_copies(self, only=None):
+        for way, kind, chunk, cut in self.parcels():
+            if only is not None and chunk != only:
+                continue
+            for step in range(0 if way == kind else 1, self.ring.reach(way, kind) + 1):
+                for turn in range(self.pairs - 1):
+                    yield self.pair_copy(way, kind, chunk, step, cut, turn)
+
+    def settle(self, only=None):
+        for copy in self.pair_copies(only):
+            copy.wait_recv()
 
     def drain(self):
-        n = self.ring.n
-        for chunk in range(self.chunks):
-            for way in range(2):
-                for step in range(n):
-                    if step < n - 1:
-                        self.ring_copy(way, chunk, step).wait_send()
-                    for at in range(self.pairs - 1):
-                        self.pair_copy(way, chunk, step, at).wait_send()
+        for copy in self.pair_copies():
+            copy.wait_send()
+        for way, kind, chunk, cut in self.parcels():
+            for step in range(self.ring.reach(way, kind)):
+                self.ring_copy(way, kind, chunk, step, cut).wait_send()
 
 
 def whole_kernel(sizes, group, tile_tokens, tile, tiles_hbm, query_hbm, vision_hbm, key_hbm, value_hbm, query_gain_hbm,
                  key_gain_hbm, grad_hbm, query_out, vision_out, key_weight, value_weight, tiles_ref, query_gain, key_gain, queries,
                  out_grad, vision, own, raw_keys,
-                 gathered, parts, held, columns, grads, leaving, arrived, total, every, mine, load_sem, own_sem,
+                 gathered, parts, held, columns, grads, leaving, arrived, total, every, mine, partial, load_sem, own_sem,
                  push_send, push_recv, mate_send, mate_recv, scatter_send, scatter_recv, leave_sem, arrive_sem, *sems):
     pairs, n, heads_cut = sizes
     ring = Ring(n)
@@ -149,6 +184,7 @@
     head_dim = key_gain.shape[1]
     model_columns = heads * head_dim
     tokens = n * rows
+    reach = n // 2
     scale = head_dim ** (-0.5)
     depth = width // CUTS
     shard = columns.shape[-1]
@@ -172,7 +208,7 @@
 
     peers = [((lane + shift // n) % pairs, (here + shift % n) % n) for shift in range(1, pairs * n)]
     mates = [(me + shift) % heads_cut for shift in range(1, heads_cut)]
-    greet([{"dp": peer[0], "seq": peer[1]} for peer in peers] + [{"mp": mate} for mate in mates])
+    all_here = greet([{"dp": peer[0], "seq": peer[1]} for peer in peers] + [{"mp": mate} for mate in mates])
     loads[0].wait()
 
     seat = me % groups
@@ -182,19 +218,31 @@
         held_in = vision if held_in is None else held_in
         return held_in.at[sample, :, pl.ds(pl.multiple_of((pair * n + index) * shard, shard), shard)]
 
-    pushes = [
-        remote(
-            columns_of(sample, *peer),
-            columns.at[lane, sample, here],
-            push_send.at[at, shift],
-            push_recv.at[at, shift],
-            {"dp": peer[0], "seq": peer[1]},
-        )
-        for at, sample in enumerate(kept)
-        for shift, peer in enumerate(peers)
-    ]
-    for copy in pushes:
-        copy.start()
+    def pushes(shift):
+        peer = (lane + shift // n) % pairs, (here + shift % n) % n
+        return [
+            remote(
+                columns_of(sample, *peer),
+                columns.at[lane, sample, here],
+                push_send.at[at, shift],
+                push_recv.at[at, shift],
+                {"dp": peer[0], "seq": peer[1]},
+            )
+            for at, sample in enumerate(kept)
+        ]
+
+    at_once = EARLY_PUSHES
+    each_time = -(-(pairs * n - 1 - at_once) // (2 * heads))
+
+    def push_some(turn):
+        for at in range(each_time):
+            shift = 1 + at_once + turn * each_time + at
+
+            @pl.when(shift < pairs * n)
+            def _():
+                for copy in pushes(shift):
+                    copy.start()
+
     mine_here = [
         pltpu.make_async_copy(
             columns_of(sample, lane, here, vision_hbm), columns.at[lane, sample, here], own_sem.at[at]
@@ -219,8 +267,9 @@
         ring,
         1,
         samples,
-        lambda way, chunk: own.at[way, chunk],
-        lambda way, chunk, whose, origin: gathered.at[way, chunk, origin],
+        heads,
+        lambda kind, chunk, cut: own.at[kind, chunk, cut],
+        lambda kind, chunk, whose, origin, cut: gathered.at[kind, chunk, origin, cut],
         sems[:4],
     )
 
@@ -241,24 +290,24 @@
         normed = (head * inverse_of(head) * key_gain[...]).astype(BF16)
         raw_keys[:, at] = head.reshape(samples, rows, head_dim)
         own[0, :, at] = normed.reshape(samples, rows, head_dim)
-    gather.start(0, 0, 0)
+    all_here()
+    gather.start(0, (0,))
+    for shift in range(1, 1 + at_once):
+        for copy in pushes(shift):
+            copy.start()
     product = project(1).astype(BF16)
     for at in range(heads):
         own[1, :, at] = product[:, at * head_dim : (at + 1) * head_dim].reshape(samples, rows, head_dim)
-    gather.start(1, 0, 0)
+    gather.start(0, (1,))
     for at in range(2):
         gathered[at, :, here] = own[at]
 
-    lag = heads
-    for step in range(1, n):
+    for step in range(1, reach + 1):
         gather.step(0, step)
-        if step == lag:
-            for way in range(2):
-                gather.start(way, 1, 0)
-        if lag < step < n - 1:
-            gather.step(1, step - lag)
-
-    def attend(sample, head):
+        if step == max(reach - 1, 1):
+            gather.start(1)
+
+    def attend(sample, head, midway):
         live = tiles_ref[:, sample : sample + 1] * tile_tokens
 
         def stacked(ref):
@@ -279,6 +328,7 @@
         probs = expo * (1.0 / jnp.sum(expo, axis=-1, keepdims=True))
         probs_b = probs.astype(BF16)
         attn = mul(probs_b, values, ((1,), (0,))).astype(BF16)
+        midway()
         delta = jnp.sum(outs.astype(F32) * attn.astype(F32), axis=-1, keepdims=True)
         dprobs = mul(outs, values, ((1,), (1,)))
         dscores = (probs * (dprobs - delta)).astype(BF16)
@@ -292,84 +342,120 @@
             cut = slice(at * head_dim, (at + 1) * head_dim)
             query_out[head, sample, :, cut] = back[at * text_rows : (at + 1) * text_rows]
 
-    def scatter_copy(way, chunk, step, block=None):
-        block = held.at[way, chunk, step] if block is None else block
-        send, recv = scatter_send.at[way, step, chunk], scatter_recv.at[way, step, chunk]
-        return remote(block, held.at[way, chunk, step], send, recv, {"seq": ring.nexts[way]})
+    def scatter_copy(way, kind, chunk, step, cut, block=None):
+        target = held.at[way, kind, chunk, step, cut]
+        at = (way, step, kind * samples + chunk, cut)
+        block = target if block is None else block
+        return remote(block, target, scatter_send.at[at], scatter_recv.at[at], {"seq": ring.nexts[way]})
 
     def scatter_start(chunk):
+        for cut in range(heads):
+            for kind in range(2):
+                for way in range(2):
+                    dest = ring.dest(way, ring.reach(way, kind))
+                    scatter_copy(way, kind, chunk, 0, cut, parts.at[kind, chunk, dest, cut]).start()
+
+    def scatter_step(chunk, step, cuts=range(heads), most=None):
+        for cut in cuts:
+            for kind in range(2):
+                for way in range(2):
+
+                    @when(step, ring.reach(way, kind), most)
+                    def _():
+                        scatter_copy(way, kind, chunk, step - 1, cut).wait_recv()
+                        block = held.at[way, kind, chunk, step - 1, cut]
+                        dest = ring.dest(way, ring.reach(way, kind) - step)
+                        summed = block[...].astype(F32) + parts[kind, chunk, dest, cut].astype(F32)
+                        block[...] = summed.astype(BF16)
+                        scatter_copy(way, kind, chunk, step, cut, block).start()
+
+    def scatter_sum(kind, chunk, cut):
+        total = parts[kind, chunk, here, cut].astype(F32)
         for way in range(2):
-            scatter_copy(way, chunk, 0, parts.at[way, chunk, ring.dest(way, 0)]).start()
-
-    def scatter_sum(way, chunk, step):
-        scatter_copy(way, chunk, step - 1).wait_recv()
-        return held[way, chunk, step - 1].astype(F32) + parts[way, chunk, ring.dest(way, step)].astype(F32)
-
-    def scatter_step(chunk, step):
-        for way in range(2):
-            held[way, chunk, step - 1] = scatter_sum(way, chunk, step).astype(BF16)
-            scatter_copy(way, chunk, step, held.at[way, chunk, step - 1]).start()
+            last = ring.reach(way, kind) - 1
+            scatter_copy(way, kind, chunk, last, cut).wait_recv()
+            total = total + held[way, kind, chunk, last, cut].astype(F32)
+        return total
 
     def scatter_last(chunk):
-        summed = scatter_sum(0, chunk, n - 1)
-        values = scatter_sum(1, chunk, n - 1)
         gain = key_gain[...]
         for at in range(heads):
             cut = slice(at * head_dim, (at + 1) * head_dim)
             raw = raw_keys[chunk, at]
-            grads[0, chunk, :, cut] = norm_back(raw, inverse_of(raw), gain, summed[at]).astype(BF16)
-            grads[1, chunk, :, cut] = values[at].astype(BF16)
+            summed = scatter_sum(0, chunk, at)
+            grads[0, chunk, :, cut] = norm_back(raw, inverse_of(raw), gain, summed).astype(BF16)
+            grads[1, chunk, :, cut] = scatter_sum(1, chunk, at).astype(BF16)
 
     for load in loads[2 + 2 * CUTS :]:
         load.wait()
 
+    early, late = range(heads - heads // 2), range(heads - heads // 2, heads)
+
     def first_sample(head, carry):
-        gather.step(1, n - 1 - lag + head)
-        attend(0, head)
+        gather.step(1, head + 1, early, heads)
+        push_some(head)
+        attend(0, head, lambda: gather.step(1, head + 1, late, heads))
         return carry
 
     lax.fori_loop(0, heads, first_sample, 0)
+    for step in range(heads + 1, reach + 1):
+        gather.step(1, step)
     scatter_start(0)
-    gather.step(1, n - 1)
-    for copy in pushes:
-        copy.wait_recv()
-    for copy in mine_here:
-        copy.wait()
-    for copy in swaps:
-        copy.start()
 
     def second_sample(head, carry):
-        scatter_step(0, head + 1)
-        attend(1, head)
+        scatter_step(0, head + 1, early, heads)
+        push_some(heads + head)
+        attend(1, head, lambda: scatter_step(0, head + 1, late, heads))
         return carry
 
     lax.fori_loop(0, heads, second_sample, 0)
+    for step in range(heads + 1, reach):
+        scatter_step(0, step)
     scatter_start(1)
+
+    row_cuts = row_cuts_of(rows)
+
+    def rows_at(cut):
+        return pl.ds(*row_cuts[cut])
 
     spread = Gather(
         ring,
         pairs,
         samples,
-        lambda way, chunk: grads.at[way, chunk],
-        lambda way, chunk, whose, origin: every.at[way, whose, chunk, origin],
+        len(row_cuts),
+        lambda kind, chunk, cut: grads.at[kind, chunk, rows_at(cut)],
+        lambda kind, chunk, whose, origin, cut: every.at[kind, whose, chunk, origin, rows_at(cut)],
         sems[4:8],
     )
-    for step in range(heads + 1, n):
-        if step < n - 1:
-            scatter_step(0, step)
+    scatter_last(0)
+    spread.start(0)
+    for step in range(1, reach + 1):
+        if step < reach:
+            scatter_step(1, step)
         else:
-            scatter_last(0)
-            for way in range(2):
-                spread.start(way, 0, 0)
-        scatter_step(1, step - heads)
-    for step in range(1, heads):
+            scatter_last(1)
+            spread.start(1)
         spread.step(0, step)
-        scatter_step(1, n - 1 - heads + step)
-    spread.step(0, heads)
-    scatter_last(1)
-    for way in range(2):
-        spread.start(way, 1, 0)
-        every[way, lane, :, here] = grads[way]
+        if step == 1:
+            for shift in range(1, pairs * n):
+                for copy in pushes(shift):
+                    copy.wait_recv()
+            for copy in mine_here:
+                copy.wait()
+            for copy in swaps:
+                copy.start()
+    for kind in range(2):
+        every[kind, lane, :, here] = grads[kind]
+    for copy in swaps:
+        copy.wait()
+    spread.settle(0)
+
+    def product(kind, sample):
+        return mul(
+            columns[:, sample].reshape(pairs * tokens, shard),
+            every[kind, :, sample].reshape(pairs * tokens, model_columns),
+            ((0,), (0,)),
+        )
 
     share = total.shape[1]
     tiles = share // tile
@@ -405,67 +491,61 @@
 
             jobs.append(job)
 
-    plan = []
-    for step in range(heads + 1, n):
-        plan.append((0, step))
-        plan.append((1, step - heads))
-    for step in range(n - heads, n - 1):
-        plan.append((1, step))
-    per_step = -(-len(jobs) // (len(plan) - 1))
-    for chunk, step in plan:
-        for _ in range(min(per_step, len(jobs))):
-            jobs.pop(0)()
-        spread.step(chunk, step)
-    for job in jobs:
-        job()
-    spread.step(1, n - 1)
-    for chunk in range(samples):
-        spread.settle(chunk, n - 1)
-
-    half = shard // 2
-
-    def rows_of(whose, origin, way):
-        return pl.ds(pl.multiple_of(((whose * n + origin) * 2 + way) * half, half), half)
+    for kind in range(2):
+
+        def job(kind=kind):
+            partial[kind] = product(kind, 0)
+
+        jobs.append(job)
+    for step in range(1, reach + 1):
+        if step < reach:
+            for _ in range(-(-len(jobs) // (reach - step))):
+                jobs.pop(0)()
+        spread.step(1, step)
+    spread.settle(1)
+
+    share_cuts = mine.shape[1]
+    cut_rows = shard // share_cuts
+
+    def rows_of(whose, origin, cut):
+        return pl.ds(pl.multiple_of(((whose * n + origin) * share_cuts + cut) * cut_rows, cut_rows), cut_rows)
 
     share_out = Gather(
         ring,
         pairs,
-        2,
-        lambda way, chunk: mine.at[chunk, way],
-        lambda way, chunk, whose, origin: weights[chunk].at[rows_of(whose, origin, way)],
+        1,
+        share_cuts,
+        lambda kind, chunk, cut: mine.at[kind, cut],
+        lambda kind, chunk, whose, origin, cut: weights[kind].at[rows_of(whose, origin, cut)],
         sems[8:],
     )
-    for copy in swaps:
-        copy.wait()
-    for chunk in range(2):
-        grad = mul(
-            columns[...].reshape(pairs * samples * tokens, shard),
-            every[chunk].reshape(pairs * samples * tokens, model_columns),
-            ((0,), (0,)),
-        ).astype(BF16)
-        mine[chunk] = grad.reshape(mine.shape[1:])
-        for way in range(2):
-            share_out.start(way, chunk, 0)
+    for kind in range(2):
+        grad = partial[kind]
+        for sample in range(1, samples):
+            grad = grad + product(kind, sample)
+        mine[kind] = grad.astype(BF16).reshape(mine.shape[1:])
+        share_out.start(0, (kind,))
     result = total[...]
     for at, copy in enumerate(copies):
         copy.wait()
         result = result + arrived[at].astype(F32)
     vision_out[...] = result.astype(BF16)
-    for chunk in range(2):
-        for way in range(2):
-            weights[chunk][rows_of(lane, here, way), :] = mine[chunk, way]
-    for step in range(1, n):
-        for chunk in range(2):
-            share_out.step(chunk, step)
-    for chunk in range(2):
-        share_out.settle(chunk, n - 1)
-
-    for copy in pushes:
-        copy.wait_send()
+    for kind in range(2):
+        for cut in range(share_cuts):
+            weights[kind][rows_of(lane, here, cut), :] = mine[kind, cut]
+    for step in range(1, reach + 1):
+        share_out.step(0, step)
+    share_out.settle()
+
+    for shift in range(1, pairs * n):
+        for copy in pushes(shift):
+            copy.wait_send()
     for chunk in range(samples):
-        for way in range(2):
-            for step in range(n - 1):
-                scatter_copy(way, chunk, step).wait_send()
+        for kind in range(2):
+            for way in range(2):
+                for step in range(ring.reach(way, kind)):
+                    for cut in range(heads):
+                        scatter_copy(way, kind, chunk, step, cut).wait_send()
     for each in (gather, spread, share_out):
         each.drain()
 
@@ -520,10 +600,16 @@
     )(query_grad, vision_grad, key_grad, value_grad)
 
 
-def ring_sems(n, pairs, chunks):
+def row_cuts_of(rows):
+    first = -(-rows // 32) * 16
+    return [(0, first), (first, rows - first)] if rows % 16 == 0 and rows > 16 else [(0, rows)]
+
+
+def ring_sems(n, pairs, chunks, cuts):
     dma = pltpu.SemaphoreType.DMA
-    pair = dma((2, n, chunks, max(pairs - 1, 1)))
-    return [dma((2, n, chunks)), dma((2, n, chunks)), pair, pair]
+    steps = n // 2
+    pair = dma((2, steps + 1, 2 * chunks, cuts, max(pairs - 1, 1)))
+    return [dma((2, steps, 2 * chunks, cuts)), dma((2, steps, 2 * chunks, cuts)), pair, pair]
 
 
 def in_hbm(array):
@@ -544,6 +630,7 @@
     groups = samples if heads_cut % samples == 0 else 1
     kept = 1 if groups > 1 else samples
     tile = 512 if share % 512 == 0 else share
+    share_cuts = 4 if shard % 64 == 0 else 1
     moved = VMEM((max(heads_cut - 1, 1), samples * rows, share), BF16)
     dma = pltpu.SemaphoreType.DMA
     hbm = pl.BlockSpec(memory_space=pltpu.HBM)
@@ -570,28 +657,29 @@
             VMEM((samples, *block), F32),
             VMEM((2, samples, n, *block), BF16),
             VMEM((2, samples, n, *block), BF16),
-            VMEM((2, samples, n - 1, *block), BF16),
+            VMEM((2, 2, samples, n // 2, *block), BF16),
             VMEM((pairs, samples, n, rows, shard), BF16),
             VMEM((2, samples, rows, columns), BF16),
             moved,
             moved,
             VMEM((samples * rows, share), F32),
             VMEM((2, pairs, samples, n, rows, columns), BF16),
-            VMEM((2, 2, shard // 2, columns), BF16),
+            VMEM((2, share_cuts, shard // share_cuts, columns), BF16),
+            VMEM((2, shard, columns), F32),
             dma((4 + 2 * CUTS + 2 * heads,)),
             dma((kept,)),
             dma((kept, pairs * n)),
             dma((kept, pairs * n)),
             dma((pairs, max(groups - 1, 1))),
             dma((pairs, max(groups - 1, 1))),
-            dma((2, n, samples)),
-            dma((2, n, samples)),
+            dma((2, n // 2, 2 * samples, heads)),
+            dma((2, n // 2, 2 * samples, heads)),
             dma((max(heads_cut - 1, 1),)),
             dma((max(heads_cut - 1, 1),)),
         ]
-        + ring_sems(n, 1, samples)
-        + ring_sems(n, pairs, samples)
-        + ring_sems(n, pairs, 2),
+        + ring_sems(n, 1, samples, heads)
+        + ring_sems(n, pairs, samples, len(row_cuts_of(rows)))
+        + ring_sems(n, pairs, 1, share_cuts),
         compiler_params=pltpu.CompilerParams(
             collective_id=1, has_side_effects=True, vmem_limit_bytes=LIMIT
         ),

time: 189 us -> 169 us (0.89)
  Pallas kernels: 188 us -> 168 us
    pallas_call x1, Pallas kernels: 180 us -> 160 us  [local(): pl.pallas_call(functools.partial(whole_kernel, sizes, group, n * rows //...]
where the time goes in v1:
time: 169 us
  Pallas kernels  168 us (99%)
    pallas_call x1, Pallas kernels, local(): pl.pallas_call(functools.partial(whole_kernel, sizes, group, n * rows //...  160 us
    pallas_call x1, Pallas kernels, emit(): pl.pallas_call(emit_kernel, out_shape=(jax.ShapeDtypeStruct((samples, tex...  7.65 us

profile of v1, /device:TPU:0, one launch (start us, length us, event | category | flops | bytes accessed | tf_op | source)
XLA Modules:
  0.0 168.5 jit_solution(12584304068467157566)
XLA Ops:
  0.6 160.1 %whole.1 = (bf16[4,2,128,512]{3,2,1,0:T(8,128)(2,1)S(1)}, bf16[160,2048]{1,0:T(8,128)(2,1)S(1)}, bf16[4096,512]{1,0:T(8,128)(2,1)S(1)}, bf16[4096,512]{1,0:T(8,128)(2,1)S(1)}) custom-call(s32[1,2]{1,0:T(1,128)} %bitcast.5, bf16[2,128,2048]{2,1,0:T(8,128)(2,1)} %query_hbm.1, bf16[2,80,4096]{2,1,0:T(8,128)(2,1)} %vision_hbm.1, bf16[4096,512]{1,0:T(8,128)(2,1)} %key_hbm.1, ...), custom_call_target="tpu_custom_call" | custom-call | flops 24999999488 | bytes 10551296 | tf_op jit(solution)/shard_map/whole/pallas_call | solution.py:639
  160.7 7.7 %emit.1 = (bf16[2,128,2048]{2,1,0:T(8,128)(2,1)}, bf16[160,2048]{1,0:T(8,128)(2,1)}, f32[4096,512]{1,0:T(8,128)}, f32[4096,512]{1,0:T(8,128)}) custom-call(bf16[4,2,128,512]{3,2,1,0:T(8,128)(2,1)S(1)} %get-tuple-element.12.query_ref, bf16[160,2048]{1,0:T(8,128)(2,1)S(1)} %get-tuple-element.13.vision_ref, bf16[4096,512]{1,0:T(8,128)(2,1)S(1)} %get-tuple-element.14.key_ref, ...), custom_call_target="tpu_custom_call" | custom-call | flops 4194304 | bytes 16777216 | tf_op jit(solution)/shard_map/emit/pallas_call | solution.py:586

commit v2 on v1

--- a/solution.py
+++ b/solution.py
@@ -69,14 +69,17 @@
         self.here = lax.axis_index("seq")
         self.place = place_of(self.here, n)
         self.nexts = (seq_of((self.place + 1) % n, n), seq_of((self.place + n - 1) % n, n))
+        self.away = {(way, step): self.at(way, step) for way in range(2) for step in range(n // 2 + 1)}
+
+    def at(self, way, away):
+        n, place = self.n, self.place
+        return seq_of((place + n - away) % n if way == 0 else (place + away) % n, n)
 
     def origin(self, way, step):
-        n, place = self.n, self.place
-        return seq_of((place + n - step) % n if way == 0 else (place + step) % n, n)
+        return self.away[way, step] if isinstance(step, int) else self.at(way, step)
 
     def dest(self, way, away):
-        n, place = self.n, self.place
-        return seq_of((place + away) % n if way == 0 else (place + n - away) % n, n)
+        return self.origin(1 - way, away)
 
     def reach(self, way, kind):
         return self.n // 2 if way == kind else self.n - 1 - self.n // 2
@@ -98,9 +101,9 @@
 
 
 class Gather:
-    def __init__(self, ring, pairs, chunks, cuts, source, target, sems):
+    def __init__(self, ring, pairs, chunks, cuts, source, target, some, sems):
         self.ring, self.pairs, self.chunks, self.cuts = ring, pairs, chunks, cuts
-        self.source, self.target, self.sems = source, target, sems
+        self.source, self.target, self.some, self.sems = source, target, some, sems
         self.lane = lax.axis_index("dp")
 
     def block(self, way, kind, chunk, step, cut):
@@ -110,13 +113,12 @@
     def ring_copy(self, way, kind, chunk, step, cut):
         at = (way, step, kind * self.chunks + chunk, cut)
         block = self.block(way, kind, chunk, step, cut)
-        return remote(*block, self.sems[0].at[at], self.sems[1].at[at], {"seq": self.ring.nexts[way]})
+        return remote(*block, self.sems[0].at[kind], self.sems[1].at[at], {"seq": self.ring.nexts[way]})
 
     def pair_copy(self, way, kind, chunk, step, cut, turn):
-        at = (way, step, kind * self.chunks + chunk, cut, turn)
         block = self.block(way, kind, chunk, step, cut)
         other = {"dp": (self.lane + 1 + turn) % self.pairs}
-        return remote(*block, self.sems[2].at[at], self.sems[3].at[at], other)
+        return remote(*block, self.sems[2].at[turn, kind], self.sems[3].at[turn, chunk, kind], other)
 
     def send(self, way, kind, chunk, step, cut, most=None):
         @when(step, self.ring.reach(way, kind), most)
@@ -143,31 +145,22 @@
                         self.ring_copy(way, kind, chunk, step - 1, cut).wait_recv()
                         self.send(way, kind, chunk, step, cut, most)
 
-    def parcels(self):
-        for chunk in range(self.chunks):
+    def settle(self, chunk):
+        near = {"seq": self.ring.nexts[0]}
+        for turn in range(self.pairs - 1):
             for kind in range(2):
-                for way in range(2):
-                    for cut in range(self.cuts):
-                        yield way, kind, chunk, cut
-
-    def pair_copies(self, only=None):
-        for way, kind, chunk, cut in self.parcels():
-            if only is not None and chunk != only:
-                continue
-            for step in range(0 if way == kind else 1, self.ring.reach(way, kind) + 1):
-                for turn in range(self.pairs - 1):
-                    yield self.pair_copy(way, kind, chunk, step, cut, turn)
-
-    def settle(self, only=None):
-        for copy in self.pair_copies(only):
-            copy.wait_recv()
+                ref = self.some(kind, 1, self.ring.n)
+                sems = self.sems[2].at[turn, kind], self.sems[3].at[turn, chunk, kind]
+                remote(ref, ref, *sems, near).wait_recv()
 
     def drain(self):
-        for copy in self.pair_copies():
-            copy.wait_send()
-        for way, kind, chunk, cut in self.parcels():
-            for step in range(self.ring.reach(way, kind)):
-                self.ring_copy(way, kind, chunk, step, cut).wait_send()
+        near = {"seq": self.ring.nexts[0]}
+        for kind in range(2):
+            sends = [(self.sems[0].at[kind], self.ring.n - 1)]
+            sends += [(self.sems[2].at[turn, kind], self.ring.n) for turn in range(self.pairs - 1)]
+            for sem, count in sends:
+                ref = self.some(kind, self.chunks, count)
+                remote(ref, ref, sem, self.sems[1].at[0, 0, 0, 0], near).wait_send()
 
 
 def whole_kernel(sizes, group, tile_tokens, tile, tiles_hbm, query_hbm, vision_hbm, key_hbm, value_hbm, query_gain_hbm,
@@ -270,6 +263,7 @@
         heads,
         lambda kind, chunk, cut: own.at[kind, chunk, cut],
         lambda kind, chunk, whose, origin, cut: gathered.at[kind, chunk, origin, cut],
+        lambda kind, chunks, count: gathered.at[kind, :chunks, :count],
         sems[:4],
     )
 
@@ -346,7 +340,7 @@
         target = held.at[way, kind, chunk, step, cut]
         at = (way, step, kind * samples + chunk, cut)
         block = target if block is None else block
-        return remote(block, target, scatter_send.at[at], scatter_recv.at[at], {"seq": ring.nexts[way]})
+        return remote(block, target, scatter_send.at[0], scatter_recv.at[at], {"seq": ring.nexts[way]})
 
     def scatter_start(chunk):
         for cut in range(heads):
@@ -425,6 +419,7 @@
         len(row_cuts),
         lambda kind, chunk, cut: grads.at[kind, chunk, rows_at(cut)],
         lambda kind, chunk, whose, origin, cut: every.at[kind, whose, chunk, origin, rows_at(cut)],
+        lambda kind, chunks, count: every.at[kind, 0, :chunks, :count],
         sems[4:8],
     )
     scatter_last(0)
@@ -517,6 +512,7 @@
         share_cuts,
         lambda kind, chunk, cut: mine.at[kind, cut],
         lambda kind, chunk, whose, origin, cut: weights[kind].at[rows_of(whose, origin, cut)],
+        lambda kind, chunks, count: weights[kind].at[: count * shard],
         sems[8:],
     )
     for kind in range(2):
@@ -535,17 +531,13 @@
             weights[kind][rows_of(lane, here, cut), :] = mine[kind, cut]
     for step in range(1, reach + 1):
         share_out.step(0, step)
-    share_out.settle()
+    share_out.settle(0)
 
     for shift in range(1, pairs * n):
         for copy in pushes(shift):
             copy.wait_send()
-    for chunk in range(samples):
-        for kind in range(2):
-            for way in range(2):
-                for step in range(ring.reach(way, kind)):
-                    for cut in range(heads):
-                        scatter_copy(way, kind, chunk, step, cut).wait_send()
+    sent = parts.at[:, :, : n - 1]
+    remote(sent, sent, scatter_send.at[0], scatter_recv.at[0, 0, 0, 0], {"seq": ring.nexts[0]}).wait_send()
     for each in (gather, spread, share_out):
         each.drain()
 
@@ -607,9 +599,8 @@
 
 def ring_sems(n, pairs, chunks, cuts):
     dma = pltpu.SemaphoreType.DMA
-    steps = n // 2
-    pair = dma((2, steps + 1, 2 * chunks, cuts, max(pairs - 1, 1)))
-    return [dma((2, steps, 2 * chunks, cuts)), dma((2, steps, 2 * chunks, cuts)), pair, pair]
+    others = max(pairs - 1, 1)
+    return [dma((2,)), dma((2, n // 2, 2 * chunks, cuts)), dma((others, 2)), dma((others, chunks, 2))]
 
 
 def in_hbm(array):
@@ -672,7 +663,7 @@
             dma((kept, pairs * n)),
             dma((pairs, max(groups - 1, 1))),
             dma((pairs, max(groups - 1, 1))),
-            dma((2, n // 2, 2 * samples, heads)),
+            dma((1,)),
             dma((2, n // 2, 2 * samples, heads)),
             dma((max(heads_cut - 1, 1),)),
             dma((max(heads_cut - 1, 1),)),

time: 169 us -> 159 us (0.941)
  Pallas kernels: 168 us -> 158 us
    pallas_call x1, Pallas kernels: 160 us -> 150 us  [local(): pl.pallas_call(functools.partial(whole_kernel, sizes, group, n * rows //...]
where the time goes in v2:
time: 159 us
  Pallas kernels  158 us (99%)
    pallas_call x1, Pallas kernels, local(): pl.pallas_call(functools.partial(whole_kernel, sizes, group, n * rows //...  150 us
    pallas_call x1, Pallas kernels, emit(): pl.pallas_call(emit_kernel, out_shape=(jax.ShapeDtypeStruct((samples, tex...  7.65 us

profile of v2, /device:TPU:0, one launch (start us, length us, event | category | flops | bytes accessed | tf_op | source)
XLA Modules:
  0.0 158.8 jit_solution(2820777595497057405)
XLA Ops:
  0.6 150.3 %whole.1 = (bf16[4,2,128,512]{3,2,1,0:T(8,128)(2,1)S(1)}, bf16[160,2048]{1,0:T(8,128)(2,1)S(1)}, bf16[4096,512]{1,0:T(8,128)(2,1)S(1)}, bf16[4096,512]{1,0:T(8,128)(2,1)S(1)}) custom-call(s32[1,2]{1,0:T(1,128)} %bitcast.5, bf16[2,128,2048]{2,1,0:T(8,128)(2,1)} %query_hbm.1, bf16[2,80,4096]{2,1,0:T(8,128)(2,1)} %vision_hbm.1, bf16[4096,512]{1,0:T(8,128)(2,1)} %key_hbm.1, ...), custom_call_target="tpu_custom_call" | custom-call | flops 24999999488 | bytes 10551296 | tf_op jit(solution)/shard_map/whole/pallas_call | solution.py:630
  151.0 7.7 %emit.1 = (bf16[2,128,2048]{2,1,0:T(8,128)(2,1)}, bf16[160,2048]{1,0:T(8,128)(2,1)}, f32[4096,512]{1,0:T(8,128)}, f32[4096,512]{1,0:T(8,128)}) custom-call(bf16[4,2,128,512]{3,2,1,0:T(8,128)(2,1)S(1)} %get-tuple-element.12.query_ref, bf16[160,2048]{1,0:T(8,128)(2,1)S(1)} %get-tuple-element.13.vision_ref, bf16[4096,512]{1,0:T(8,128)(2,1)S(1)} %get-tuple-element.14.key_ref, ...), custom_call_target="tpu_custom_call" | custom-call | flops 4194304 | bytes 16777216 | tf_op jit(solution)/shard_map/emit/pallas_call | solution.py:578

commit v3 on v2

--- a/solution.py
+++ b/solution.py
@@ -196,7 +196,8 @@
             later.append((source.at[:, :, head * wide : (head + 1) * wide], target.at[head]))
     for at, (source, target) in enumerate(later):
         loads.append(pltpu.make_async_copy(source, target, load_sem.at[1 + 2 * CUTS + at]))
-    for load in loads:
+    small = loads[1 + 2 * CUTS : 4 + 2 * CUTS]
+    for load in small + loads[: 1 + 2 * CUTS] + loads[4 + 2 * CUTS :]:
         load.start()
 
     peers = [((lane + shift // n) % pairs, (here + shift % n) % n) for shift in range(1, pairs * n)]
@@ -585,7 +586,7 @@
         ),
         in_specs=[pl.BlockSpec(memory_space=VMEM)] * 4,
         out_specs=(pl.BlockSpec(memory_space=pltpu.HBM),) * 4,
-        scratch_shapes=[VMEM((4, block, columns), F32), dma((4,)), dma((heads + 1,))],
+        scratch_shapes=[VMEM((8, block, columns), F32), dma((8,)), dma((heads + 1,))],
         compiler_params=pltpu.CompilerParams(vmem_limit_bytes=16 * 1024 * 1024),
         cost_estimate=pl.CostEstimate(flops=2 * rows * columns, bytes_accessed=8 * rows * columns, transcendentals=0),
         name="emit",

time: 159 us -> 157 us (0.987)
  Pallas kernels: 158 us -> 156 us
where the time goes in v3:
time: 157 us
  Pallas kernels  156 us (99%)
    pallas_call x1, Pallas kernels, local(): pl.pallas_call(functools.partial(whole_kernel, sizes, group, n * rows //...  150 us
    pallas_call x1, Pallas kernels, emit(): pl.pallas_call(emit_kernel, out_shape=(jax.ShapeDtypeStruct((samples, tex...  6.43 us

profile of v3, /device:TPU:0, one launch (start us, length us, event | category | flops | bytes accessed | tf_op | source)
XLA Modules:
  0.0 157.2 jit_solution(4909385271794587648)
XLA Ops:
  0.6 150.0 %whole.1 = (bf16[4,2,128,512]{3,2,1,0:T(8,128)(2,1)S(1)}, bf16[160,2048]{1,0:T(8,128)(2,1)S(1)}, bf16[4096,512]{1,0:T(8,128)(2,1)S(1)}, bf16[4096,512]{1,0:T(8,128)(2,1)S(1)}) custom-call(s32[1,2]{1,0:T(1,128)} %bitcast.5, bf16[2,128,2048]{2,1,0:T(8,128)(2,1)} %query_hbm.1, bf16[2,80,4096]{2,1,0:T(8,128)(2,1)} %vision_hbm.1, bf16[4096,512]{1,0:T(8,128)(2,1)} %key_hbm.1, ...), custom_call_target="tpu_custom_call" | custom-call | flops 24999999488 | bytes 10551296 | tf_op jit(solution)/shard_map/whole/pallas_call | solution.py:631
  150.6 6.4 %emit.1 = (bf16[2,128,2048]{2,1,0:T(8,128)(2,1)}, bf16[160,2048]{1,0:T(8,128)(2,1)}, f32[4096,512]{1,0:T(8,128)}, f32[4096,512]{1,0:T(8,128)}) custom-call(bf16[4,2,128,512]{3,2,1,0:T(8,128)(2,1)S(1)} %get-tuple-element.12.query_ref, bf16[160,2048]{1,0:T(8,128)(2,1)S(1)} %get-tuple-element.13.vision_ref, bf16[4096,512]{1,0:T(8,128)(2,1)S(1)} %get-tuple-element.14.key_ref, ...), custom_call_target="tpu_custom_call" | custom-call | flops 4194304 | bytes 16777216 | tf_op jit(solution)/shard_map/emit/pallas_call | solution.py:579
